TPU v7x, 512 devices: a whole 4x8x8 slice. The times are simulated.
512 devices in a mesh: gx: 16 (over y, z_lo), gy: 32 (over x, z_hi, core).
Axes of the slice: x: 4, y: 8, z: 8 (z_hi: 4, z_lo: 2; z = z_hi * 2 + z_lo), core: 2. Of those that a mesh axis runs over, the one named last changes fastest.
Arguments:
- fields: bfloat16 [8, 256, 512, 192], P(None, 'gx', 'gy'), may hold values from -6 to 6
- gain_window: float32 [192], replicated, may hold values from 0.1 to 1.9
- mixer_fine: bfloat16 [192, 576], replicated, may hold values from -3 to 3
- output_fine: bfloat16 [192, 192], replicated, may hold values from -0.4375 to 0.4375
- gain_hidden: float32 [192], replicated, may hold values from 0.1 to 1.9
- expand: bfloat16 [192, 768], replicated, may hold values from -0.4375 to 0.4375
- contract: bfloat16 [768, 192], replicated, may hold values from -0.21875 to 0.21875
- gain_merge: float32 [768], replicated, may hold values from 0.1 to 1.9
- merge_weight: bfloat16 [768, 384], replicated, may hold values from -0.21875 to 0.21875
- gain_coarse: float32 [384], replicated, may hold values from 0.1 to 1.9
- mixer_coarse: bfloat16 [384, 1152], replicated, may hold values from -2.1 to 2.1
- output_coarse: bfloat16 [384, 384], replicated, may hold values from -0.3125 to 0.3125
Outputs:
- merged: bfloat16 [8, 128, 256, 384], P(None, 'gx', 'gy')
- coarse: bfloat16 [8, 128, 256, 384], P(None, 'gx', 'gy')
All inputs are finite; a program needn't handle non-finite values.
Results may differ from a plain program's by a relative error of at most 0.019.
Values may be sent and summed in bfloat16 or wider, within the bound.
No kernel may reach another device: no remote copies, remote signals or barrier semaphores. Data moves between devices by JAX's collectives and lax.ppermute only.
A program may use at most 128 MiB of HBM per device.

v0:
```python
import functools
import math

import jax
import jax.numpy as jnp
from jax import lax
from jax.experimental import pallas as pl
from jax.experimental.pallas import tpu as pltpu
from jax.sharding import PartitionSpec as P


HEAD = 32
EPS = 1e-05
SCALE = math.log2(math.e) / math.sqrt(HEAD)
F32 = jnp.float32
BF16 = jnp.bfloat16


def dot(a, b):
    return jnp.dot(a, b, preferred_element_type=F32)


def dot_nt(a, b):
    return lax.dot_general(a, b, (((1,), (1,)), ((), ())), preferred_element_type=F32)


def iota(shape, dim):
    return lax.broadcasted_iota(jnp.int32, shape, dim)


def one_hot(rows, source):
    return jnp.where(iota((rows, rows), 1) == source, 1.0, 0.0).astype(BF16)


def normalize(values, scaling):
    center = values - jnp.mean(values, -1, keepdims=True)
    spread = jnp.mean(center * center, -1, keepdims=True)
    return center * lax.rsqrt(spread + EPS) * scaling


def pack_body(odd_ref, x_ref, own_ref, col_ref, row_ref, diag_ref, order_ref):
    @pl.when(pl.program_id(0) == 0)
    def _():
        odd = odd_ref[0]
        place = iota((256, 256), 0)
        piece = place // 64
        phase = (place // 16) % 4
        i = 2 * ((place // 4) % 4) + phase % 2
        j = 2 * (place % 4) + phase // 2
        bottom = jnp.where(piece < 2, 1, 0)
        keep = jnp.where((piece == 0) | (piece == 3), odd, 1 - odd)
        order_ref[...] = one_hot(256, (8 * bottom + i) * 16 + 8 * keep + j)

    samples = x_ref.shape[0]
    for n in range(samples):
        tokens = x_ref[n].reshape(256, 192)
        sorted_tokens = dot(order_ref[...], tokens)
        own_ref[n] = sorted_tokens[:64].astype(BF16)
        for slot, ref in enumerate((col_ref, row_ref, diag_ref)):
            part = sorted_tokens[64 * (slot + 1) : 64 * (slot + 2)]
            ref[n, :64, :] = part[:, :128].astype(BF16)
            ref[n, 64:, :] = jnp.concatenate([part[:32, 128:], part[32:, 128:]], 1).astype(BF16)


def pack(odd, fields):
    samples = fields.shape[0]
    step = 2
    piece = jax.ShapeDtypeStruct((samples, 96, 128), BF16)
    piece_spec = pl.BlockSpec((step, 96, 128), lambda n: (n, 0, 0))
    return pl.pallas_call(
        pack_body,
        grid=(samples // step,),
        in_specs=[
            pl.BlockSpec(memory_space=pltpu.SMEM),
            pl.BlockSpec((step, 16, 16, 192), lambda n: (n, 0, 0, 0)),
        ],
        out_specs=[pl.BlockSpec((step, 64, 192), lambda n: (n, 0, 0))] + [piece_spec] * 3,
        out_shape=[jax.ShapeDtypeStruct((samples, 64, 192), BF16)] + [piece] * 3,
        scratch_shapes=[pltpu.VMEM((256, 256), BF16)],
        compiler_params=pltpu.CompilerParams(vmem_limit_bytes=16 << 20),
        name="pack",
    )(odd, fields)


def unpack(ref, n):
    low = ref[n, :64, :].astype(F32)
    high = ref[n, 64:, :].astype(F32)
    turned = pltpu.roll(high, 64, 1)
    return jnp.concatenate([low, jnp.concatenate([high, turned], 0)[:, :64]], 1)


def head_mask(head, last):
    lane = iota((1, 128), 1) // HEAD
    return jnp.where(jnp.minimum(lane, last) == head, 1.0, 0.0).astype(BF16)


def attend_group(queries, keys, values, heads):
    rows = queries.shape[0]
    length = keys.shape[0]
    masks = [head_mask(head, heads - 1) for head in range(heads)]
    scores = dot_nt(jnp.concatenate([queries * mask for mask in masks], 0), keys)
    highest = jnp.max(scores, -1, keepdims=True) * SCALE
    power = jnp.exp2(scores * SCALE - highest).astype(BF16)
    parts = range(heads)
    powers = [power[head * rows : (head + 1) * rows] for head in parts]
    weights = [
        jnp.concatenate([values * mask, jnp.broadcast_to(mask, (length, 128))], 1) for mask in masks
    ]
    sums = dot(jnp.concatenate(powers, 1), jnp.concatenate(weights, 0))
    return highest, masks, sums[:, :128], sums[:, 128:]


def attend_whole(queries, keys, values, heads):
    _, _, weighted, total = attend_group(queries, keys, values, heads)
    return (weighted / total).astype(BF16)


def attend_part(queries, keys, values, heads):
    rows = queries.shape[0]
    highest, masks, weighted, total = attend_group(queries, keys, values, heads)
    top = sum(
        highest[head * rows : (head + 1) * rows] * masks[head].astype(F32) for head in range(heads)
    )
    return top, weighted, total


def gelu(x):
    return 0.5 * x * (1.0 + lax.erf(x * math.sqrt(0.5)))


def fine_body(
    own_ref,
    col_ref,
    row_ref,
    diag_ref,
    gain_window,
    mixer,
    output,
    gain_hidden,
    expand,
    contract,
    gain_merge,
    merge_weight,
    own_out,
    col_out,
    row_out,
    diag_out,
):
    windows = own_ref.shape[0]
    tokens = jnp.concatenate(
        [
            part
            for n in range(windows)
            for part in (
                own_ref[n].astype(F32),
                unpack(col_ref, n),
                unpack(row_ref, n),
                unpack(diag_ref, n),
            )
        ],
        0,
    )
    normed = normalize(tokens, gain_window[...]).astype(BF16)
    mixed = dot(normed, mixer[...]).astype(BF16)
    contexts = []
    for n in range(windows):
        one = mixed[256 * n : 256 * (n + 1)]
        contexts.append(
            jnp.concatenate(
                [
                    attend_whole(one[:, :128], one[:, 256:384], one[:, 512:640], 4),
                    attend_whole(one[:, 128:256], one[:, 384:512], one[:, 640:], 2),
                ],
                1,
            )
        )
    context = jnp.concatenate(contexts, 0)
    attended = (tokens + dot(context, output[...])).astype(BF16).astype(F32)
    normed = normalize(attended, gain_hidden[...]).astype(BF16)
    hidden = gelu(dot(normed, expand[...])).astype(BF16)
    refined = (attended + dot(hidden, contract[...])).astype(BF16).astype(F32)
    phases = [
        jnp.concatenate(
            [
                refined[64 * piece + 16 * k : 64 * piece + 16 * (k + 1)]
                for piece in range(4 * windows)
            ],
            0,
        )
        for k in range(4)
    ]
    mean = sum(jnp.sum(part, -1, keepdims=True) for part in phases) / 768.0
    centers = [part - mean for part in phases]
    spread = sum(jnp.sum(part * part, -1, keepdims=True) for part in centers) / 768.0
    ratio = lax.rsqrt(spread + EPS)
    merged = sum(
        dot((centers[k] * ratio * gain_merge[k : k + 1, :]).astype(BF16), merge_weight[k])
        for k in range(4)
    ).astype(BF16)
    for n in range(windows):
        for slot, ref in enumerate((own_out, col_out, row_out, diag_out)):
            ref[n] = merged[64 * n + 16 * slot : 64 * n + 16 * (slot + 1)]


def whole(array):
    return pl.BlockSpec(array.shape, lambda n: (0,) * array.ndim)


def fine(own, col, row, diag, *weights):
    samples = own.shape[0]
    step = 4
    piece_spec = pl.BlockSpec((step, 96, 128), lambda n: (n, 0, 0))
    return pl.pallas_call(
        fine_body,
        grid=(samples // step,),
        in_specs=[pl.BlockSpec((step, 64, 192), lambda n: (n, 0, 0))]
        + [piece_spec] * 3
        + [whole(w) for w in weights],
        out_specs=[pl.BlockSpec((step, 16, 384), lambda n: (n, 0, 0))] * 4,
        out_shape=[jax.ShapeDtypeStruct((samples, 16, 384), BF16)] * 4,
        compiler_params=pltpu.CompilerParams(vmem_limit_bytes=32 << 20),
        name="fine",
    )(own, col, row, diag, *weights)


def assemble_body(odd_ref, own_ref, col_ref, row_ref, diag_ref, out_ref):
    odd = odd_ref[0]
    place = iota((64, 64), 0)
    r = place // 8
    c = place % 8
    bottom = r // 4
    keep = jnp.where(c // 4 == odd, 1, 0)
    piece = jnp.where(bottom == 1, 1 - keep, 2 + keep)
    order = one_hot(64, piece * 16 + (r % 4) * 4 + c % 4)
    for n in range(own_ref.shape[0]):
        parts = jnp.concatenate([own_ref[n], col_ref[n], row_ref[n], diag_ref[n]], 0)
        out_ref[n] = dot(order, parts).astype(BF16)


def assemble(odd, *pieces):
    samples = pieces[0].shape[0]
    vmem = pl.BlockSpec(memory_space=pltpu.VMEM)
    return pl.pallas_call(
        assemble_body,
        in_specs=[pl.BlockSpec(memory_space=pltpu.SMEM)] + [vmem] * 4,
        out_specs=vmem,
        out_shape=jax.ShapeDtypeStruct((samples, 64, 384), BF16),
        compiler_params=pltpu.CompilerParams(vmem_limit_bytes=8 << 20),
        name="assemble",
    )(odd, *pieces)


def group(values, n, rows, g):
    return values[rows * n : rows * (n + 1), 128 * g : 128 * (g + 1)]


def coarse_first_body(mine_ref, twin_ref, gain, mixer, query_ref, top_ref, sum_ref, total_ref):
    windows = mine_ref.shape[0]
    tokens = jnp.concatenate(
        [ref[n].astype(F32) for ref in (mine_ref, twin_ref) for n in range(windows)], 0
    )
    normed = normalize(tokens, gain[...]).astype(BF16)
    queries = dot(normed[: 64 * windows], mixer[:, :384]).astype(BF16)
    pairs = dot(normed, mixer[:, 384:]).astype(BF16)
    for n in range(windows):
        query_ref[n] = queries[64 * n : 64 * (n + 1)]
        held = jnp.concatenate(
            [pairs[64 * k : 64 * (k + 1)] for k in (n, n + windows)], 0
        )
        for g in range(3):
            lanes = slice(128 * g, 128 * (g + 1))
            top, weighted, total = attend_part(
                group(queries, n, 64, g), group(held, 0, 128, g), group(held, 0, 128, g + 3), 4
            )
            top_ref[n, :, lanes] = top
            sum_ref[n, :, lanes] = weighted
            total_ref[n, :, lanes] = total


def coarse_second_body(
    mine_ref, a_ref, b_ref, query_ref, top_ref, sum_ref, total_ref, gain, mixer, output, out_ref
):
    windows = mine_ref.shape[0]
    tokens = jnp.concatenate(
        [ref[n].astype(F32) for n in range(windows) for ref in (a_ref, b_ref)], 0
    )
    normed = normalize(tokens, gain[...]).astype(BF16)
    pairs = dot(normed, mixer[:, 384:]).astype(BF16)
    contexts = []
    for n in range(windows):
        parts = []
        for g in range(3):
            lanes = slice(128 * g, 128 * (g + 1))
            top, weighted, total = attend_part(
                query_ref[n, :, lanes], group(pairs, n, 128, g), group(pairs, n, 128, g + 3), 4
            )
            before = top_ref[n, :, lanes]
            highest = jnp.maximum(before, top)
            old = jnp.exp2(before - highest)
            new = jnp.exp2(top - highest)
            weighted = sum_ref[n, :, lanes] * old + weighted * new
            total = total_ref[n, :, lanes] * old + total * new
            parts.append((weighted / total).astype(BF16))
        contexts.append(jnp.concatenate(parts, 1))
    update = dot(jnp.concatenate(contexts, 0), output[...])
    for n in range(windows):
        mine = mine_ref[n].astype(F32)
        out_ref[n] = (mine + update[64 * n : 64 * (n + 1)]).astype(BF16)


def coarse_call(body, step, tiles, weights, kinds):
    samples = tiles[0].shape[0]
    spec = pl.BlockSpec((step, 64, 384), lambda n: (n, 0, 0))
    shapes = [jax.ShapeDtypeStruct((samples, 64, 384), kind) for kind in kinds]
    return pl.pallas_call(
        body,
        grid=(samples // step,),
        in_specs=[spec] * len(tiles) + [whole(w) for w in weights],
        out_specs=[spec] * len(kinds),
        out_shape=shapes,
        compiler_params=pltpu.CompilerParams(vmem_limit_bytes=24 << 20),
        cost_estimate=pl.CostEstimate(
            flops=2_000_000_000, transcendentals=1_000_000, bytes_accessed=4_000_000
        ),
    )(*tiles, *weights)


def shards(
    rows,
    columns,
    fields,
    gain_window,
    mixer_fine,
    output_fine,
    gain_hidden,
    expand,
    contract,
    gain_merge,
    merge_weight,
    gain_coarse,
    mixer_coarse,
    output_coarse,
):
    samples = fields.shape[0]

    def moved(value, target, back=False):
        pairs = []
        for p in range(rows):
            for q in range(columns):
                to_p, to_q = target(p, q)
                pair = (p * columns + q, (to_p % rows) * columns + to_q % columns)
                pairs.append(pair[::-1] if back else pair)
        return lax.ppermute(value, ("gx", "gy"), pairs)

    def to_row(p, q):
        return p - 1, q

    def to_col(p, q):
        return p, q - 1 if p % 2 else q + 1

    def to_diag(p, q):
        return p - 1, q + 1 if p % 2 else q - 1

    odd = (lax.axis_index("gx") % 2).astype(jnp.int32).reshape(1)
    own, col, row, diag = pack(odd, fields)
    row = moved(row, to_row)
    diag = moved(diag, to_diag)
    col = moved(col, to_col)
    mixer = jnp.pad(mixer_fine.reshape(192, 3, 192), ((0, 0), (0, 0), (0, 64))).reshape(192, 768)
    own, col, row, diag = fine(
        own,
        col,
        row,
        diag,
        gain_window.reshape(1, 192),
        mixer,
        jnp.pad(output_fine, ((0, 64), (0, 0))),
        gain_hidden.reshape(1, 192),
        expand,
        contract,
        gain_merge.reshape(4, 192),
        merge_weight.reshape(4, 192, 384),
    )
    row = moved(row, to_row, True)
    diag = moved(diag, to_diag, True)
    col = moved(col, to_col, True)
    tile = assemble(odd, own, col, row, diag)
    beside = moved(tile, lambda p, q: (p ^ 1, q))
    twin = moved(tile, lambda p, q: (p, q ^ 1))
    gain = gain_coarse.reshape(1, 384)
    first = coarse_call(
        coarse_first_body, 4, (tile, twin), (gain, mixer_coarse), (BF16, F32, F32, F32)
    )
    beyond = moved(beside, lambda p, q: (p, q ^ 1))
    (result,) = coarse_call(
        coarse_second_body,
        4,
        (tile, beside, beyond, *first),
        (gain, mixer_coarse, output_coarse),
        (BF16,),
    )
    shape = (samples, 8, 8, 384)
    return tile.reshape(shape), result.reshape(shape)


def solution(mesh):
    place = P(None, "gx", "gy", None)
    body = functools.partial(shards, mesh.shape["gx"], mesh.shape["gy"])
    return jax.shard_map(
        body, mesh=mesh, in_specs=(place,) + (P(),) * 11, out_specs=(place, place), check_vma=False
    )
```

profile of v0, /device:TPU:1, one launch (start us, length us, event | category | flops | bytes accessed | tf_op | source)
XLA Modules:
  0.0 88.0 jit_solution(12458865902466418431)
XLA Ops:
  0.7 1.2 %copy-done = bf16[8,16,16,192]{3,2,1,0:T(8,128)(2,1)S(1)} copy-done((bf16[8,16,16,192]{3,2,1,0:T(8,128)(2,1)S(1)}, bf16[8,16,16,192]{3,2,1,0:T(8,128)(2,1)}, u32[]{:S(2)}) %copy-start) | copy-done | bytes 786456
  1.9 1.3 %pack.1 = (bf16[8,64,192]{2,1,0:T(8,128)(2,1)S(1)}, bf16[8,96,128]{2,1,0:T(8,128)(2,1)S(1)}, bf16[8,96,128]{2,1,0:T(8,128)(2,1)S(1)}, bf16[8,96,128]{2,1,0:T(8,128)(2,1)S(1)}) custom-call(s32[1]{0:T(128)} %bitcast.odd_ref, bf16[8,16,16,192]{3,2,1,0:T(8,128)(2,1)S(1)} %copy-done), custom_call_target="tpu_custom_call" | custom-call | tf_op jit(solution)/shard_map/pack/pallas_call | solution.py:70
  3.2 7.2 %collective-permute-start = (bf16[8,96,128]{2,1,0:T(8,128)(2,1)S(1)}, bf16[8,96,128]{2,1,0:T(8,128)(2,1)S(1)}, u32[]{:S(2)}, u32[]{:S(2)}) collective-permute-start(bf16[8,96,128]{2,1,0:T(8,128)(2,1)S(1)} %get-tuple-element.15), channel_id=1, source_target_pairs={{0,1},{1,2},{2,3},{3,4},{4,5},{5,6},{6,7},{7,8},{8,9},{9,10},{10,1... | collective-permute-start | bytes 589832 | tf_op jit(solution)/shard_map/ppermute | solution.py:353
  10.4 3.1 %collective-permute-start.1 = (bf16[8,96,128]{2,1,0:T(8,128)(2,1)S(1)}, bf16[8,96,128]{2,1,0:T(8,128)(2,1)S(1)}, u32[]{:S(2)}, u32[]{:S(2)}) collective-permute-start(bf16[8,96,128]{2,1,0:T(8,128)(2,1)S(1)} %get-tuple-element.16), channel_id=1, source_target_pairs={{0,480},{1,481},{2,482},{3,483},{4,484},{5,485},{6,486},{7,487},{8... | collective-permute-start | bytes 589832 | tf_op jit(solution)/shard_map/ppermute | solution.py:353
  13.5 11.6 %collective-permute-start.2 = (bf16[8,96,128]{2,1,0:T(8,128)(2,1)S(1)}, bf16[8,96,128]{2,1,0:T(8,128)(2,1)S(1)}, u32[]{:S(2)}, u32[]{:S(2)}) collective-permute-start(bf16[8,96,128]{2,1,0:T(8,128)(2,1)S(1)} %get-tuple-element.17), channel_id=1, source_target_pairs={{0,511},{1,480},{2,481},{3,482},{4,483},{5,484},{6,485},{7,486},{8... | collective-permute-start | bytes 589832 | tf_op jit(solution)/shard_map/ppermute | solution.py:353
  25.5 0.8 copy-done.9
  26.3 0.2 copy.17.contract
  26.6 0.7 copy-done.12
  27.4 2.5 %collective-permute-done.2.diag_ref = bf16[8,96,128]{2,1,0:T(8,128)(2,1)S(1)} collective-permute-done((bf16[8,96,128]{2,1,0:T(8,128)(2,1)S(1)}, bf16[8,96,128]{2,1,0:T(8,128)(2,1)S(1)}, u32[]{:S(2)}, u32[]{:S(2)}) %collective-permute-start.2) | collective-permute-done | bytes 196640 | tf_op jit(solution)/shard_map/ppermute | solution.py:353
  29.8 0.7 copy-done.5
  30.5 10.7 %fine.1 = (bf16[8,16,384]{2,1,0:T(8,128)(2,1)S(1)}, bf16[8,16,384]{2,1,0:T(8,128)(2,1)S(1)}, bf16[8,16,384]{2,1,0:T(8,128)(2,1)S(1)}, bf16[8,16,384]{2,1,0:T(8,128)(2,1)S(1)}) custom-call(bf16[8,64,192]{2,1,0:T(8,128)(2,1)S(1)} %get-tuple-element.14.own_ref, bf16[8,96,128]{2,1,0:T(8,128)(2,1)S(1)} %collective-permute-done.col_ref, ...), custom_call_target="tpu_custom_call" | custom-call | tf_op jit(solution)/shard_map/fine/pallas_call | solution.py:213
  41.2 6.0 %collective-permute-start.3 = (bf16[8,16,384]{2,1,0:T(8,128)(2,1)S(1)}, bf16[8,16,384]{2,1,0:T(8,128)(2,1)S(1)}, u32[]{:S(2)}, u32[]{:S(2)}) collective-permute-start(bf16[8,16,384]{2,1,0:T(8,128)(2,1)S(1)} %get-tuple-element.19), channel_id=1, source_target_pairs={{1,0},{2,1},{3,2},{4,3},{5,4},{6,5},{7,6},{8,7},{9,8},{10,9},{11,1... | collective-permute-start | bytes 294920 | tf_op jit(solution)/shard_map/ppermute | solution.py:353
  47.3 1.9 %collective-permute-start.4 = (bf16[8,16,384]{2,1,0:T(8,128)(2,1)S(1)}, bf16[8,16,384]{2,1,0:T(8,128)(2,1)S(1)}, u32[]{:S(2)}, u32[]{:S(2)}) collective-permute-start(bf16[8,16,384]{2,1,0:T(8,128)(2,1)S(1)} %get-tuple-element.20), channel_id=1, source_target_pairs={{480,0},{481,1},{482,2},{483,3},{484,4},{485,5},{486,6},{487,7},{4... | collective-permute-start | bytes 294920 | tf_op jit(solution)/shard_map/ppermute | solution.py:353
  49.2 1.9 %collective-permute-start.5 = (bf16[8,16,384]{2,1,0:T(8,128)(2,1)S(1)}, bf16[8,16,384]{2,1,0:T(8,128)(2,1)S(1)}, u32[]{:S(2)}, u32[]{:S(2)}) collective-permute-start(bf16[8,16,384]{2,1,0:T(8,128)(2,1)S(1)} %get-tuple-element.21), channel_id=1, source_target_pairs={{511,0},{480,1},{481,2},{482,3},{483,4},{484,5},{485,6},{486,7},{4... | collective-permute-start | bytes 294920 | tf_op jit(solution)/shard_map/ppermute | solution.py:353
  51.1 4.5 %collective-permute-done.4.row_ref = bf16[8,16,384]{2,1,0:T(8,128)(2,1)S(1)} collective-permute-done((bf16[8,16,384]{2,1,0:T(8,128)(2,1)S(1)}, bf16[8,16,384]{2,1,0:T(8,128)(2,1)S(1)}, u32[]{:S(2)}, u32[]{:S(2)}) %collective-permute-start.4) | collective-permute-done | bytes 98336 | tf_op jit(solution)/shard_map/ppermute | solution.py:353
  55.6 2.3 %collective-permute-done.5.diag_ref = bf16[8,16,384]{2,1,0:T(8,128)(2,1)S(1)} collective-permute-done((bf16[8,16,384]{2,1,0:T(8,128)(2,1)S(1)}, bf16[8,16,384]{2,1,0:T(8,128)(2,1)S(1)}, u32[]{:S(2)}, u32[]{:S(2)}) %collective-permute-start.5) | collective-permute-done | bytes 98336 | tf_op jit(solution)/shard_map/ppermute | solution.py:353
  57.9 1.0 %assemble.1.mine_ref = bf16[8,64,384]{2,1,0:T(8,128)(2,1)} custom-call(s32[1]{0:T(128)} %bitcast.odd_ref, bf16[8,16,384]{2,1,0:T(8,128)(2,1)S(1)} %get-tuple-element.18.own_ref, bf16[8,16,384]{2,1,0:T(8,128)(2,1)S(1)} %collective-permute-done.3.col_ref, bf16[8,16,384]{2,1,0:T(8,128)(2,1)S(1)} %collective-permute-done.4.row_ref, ...), custom_call_target="tpu_custom_call" | custom-call | tf_op jit(solution)/shard_map/assemble/pallas_call | solution.py:243
  58.9 1.9 %collective-permute-start.6 = (bf16[8,64,384]{2,1,0:T(8,128)(2,1)}, bf16[8,64,384]{2,1,0:T(8,128)(2,1)S(1)}, u32[]{:S(2)}, u32[]{:S(2)}) collective-permute-start(bf16[8,64,384]{2,1,0:T(8,128)(2,1)} %assemble.1.mine_ref), channel_id=1, source_target_pairs={{0,32},{1,33},{2,34},{3,35},{4,36},{5,37},{6,38},{7,39},{8,40},{9,... | collective-permute-start | bytes 1179656 | tf_op jit(solution)/shard_map/ppermute | solution.py:353
  60.8 4.6 %collective-permute-start.8 = (bf16[8,64,384]{2,1,0:T(8,128)(2,1)}, bf16[8,64,384]{2,1,0:T(8,128)(2,1)S(1)}, u32[]{:S(2)}, u32[]{:S(2)}) collective-permute-start(bf16[8,64,384]{2,1,0:T(8,128)(2,1)} %assemble.1.mine_ref), channel_id=1, source_target_pairs={{0,1},{1,0},{2,3},{3,2},{4,5},{5,4},{6,7},{7,6},{8,9},{9,8},{10,11... | collective-permute-start | bytes 1179656 | tf_op jit(solution)/shard_map/ppermute | solution.py:353
  65.4 3.6 %collective-permute-done.6.a_ref = bf16[8,64,384]{2,1,0:T(8,128)(2,1)S(1)} collective-permute-done((bf16[8,64,384]{2,1,0:T(8,128)(2,1)}, bf16[8,64,384]{2,1,0:T(8,128)(2,1)S(1)}, u32[]{:S(2)}, u32[]{:S(2)}) %collective-permute-start.6) | collective-permute-done | bytes 393248 | tf_op jit(solution)/shard_map/ppermute | solution.py:353
  69.0 5.4 %collective-permute-start.7 = (bf16[8,64,384]{2,1,0:T(8,128)(2,1)S(1)}, bf16[8,64,384]{2,1,0:T(8,128)(2,1)S(1)}, u32[]{:S(2)}, u32[]{:S(2)}) collective-permute-start(bf16[8,64,384]{2,1,0:T(8,128)(2,1)S(1)} %collective-permute-done.6.a_ref), channel_id=1, source_target_pairs={{0,1},{1,0},{2,3},{3,2},{4,5},{5,4},{6,7},{7,6},{8,9},{9,8},{10,11... | collective-permute-start | bytes 1179656 | tf_op jit(solution)/shard_map/ppermute | solution.py:353
  74.5 1.0 %copy-done.2 = bf16[8,64,384]{2,1,0:T(8,128)(2,1)S(1)} copy-done((bf16[8,64,384]{2,1,0:T(8,128)(2,1)S(1)}, bf16[8,64,384]{2,1,0:T(8,128)(2,1)}, u32[]{:S(2)}) %copy-start.2) | copy-done | bytes 393240
  75.5 5.7 %shard_map.131 = (bf16[8,64,384]{2,1,0:T(8,128)(2,1)S(1)}, f32[8,64,384]{2,1,0:T(8,128)S(1)}, f32[8,64,384]{2,1,0:T(8,128)S(1)}, f32[8,64,384]{2,1,0:T(8,128)S(1)}) custom-call(bf16[8,64,384]{2,1,0:T(8,128)(2,1)S(1)} %copy-done.2, bf16[8,64,384]{2,1,0:T(8,128)(2,1)S(1)} %collective-permute-done.8.twin_ref, f32[1,384]{1,0:T(1,128)S(1)} %reshape.42.gain, ...), custom_call_target="tpu_custom_call" | custom-call | flops 2000000000 | bytes 4000000 | tf_op jit(solution)/shard_map/pallas_call | solution.py:315
  81.2 6.8 %shard_map.132 = bf16[8,64,384]{2,1,0:T(8,128)(2,1)} custom-call(bf16[8,64,384]{2,1,0:T(8,128)(2,1)S(1)} %copy-done.3, bf16[8,64,384]{2,1,0:T(8,128)(2,1)S(1)} %collective-permute-done.6.a_ref, bf16[8,64,384]{2,1,0:T(8,128)(2,1)S(1)} %collective-permute-done.7.b_ref, bf16[8,64,384]{2,1,0:T(8,128)(2,1)S(1)} %get-tuple-element.22.query_ref, ...), custom_call_target="tpu_custom_call" | custom-call | flops 2000000000 | bytes 4000000 | tf_op jit(solution)/shard_map/pallas_call | solution.py:315
  (34 shorter events, 0.5 us)
Async XLA Ops:
  0.6 1.2 %copy-start = (bf16[8,16,16,192]{3,2,1,0:T(8,128)(2,1)S(1)}, bf16[8,16,16,192]{3,2,1,0:T(8,128)(2,1)}, u32[]{:S(2)}) copy-start(bf16[8,16,16,192]{3,2,1,0:T(8,128)(2,1)} %x_ref.1) | copy-start | bytes 2359300
  1.9 23.3 %copy-start.10 = (bf16[192,576]{1,0:T(8,128)(2,1)S(1)}, bf16[192,576]{1,0:T(8,128)(2,1)}, u32[]{:S(2)}) copy-start(bf16[192,576]{1,0:T(8,128)(2,1)} %param.14) | copy-start | bytes 663556
  3.2 24.1 %collective-permute-start = (bf16[8,96,128]{2,1,0:T(8,128)(2,1)S(1)}, bf16[8,96,128]{2,1,0:T(8,128)(2,1)S(1)}, u32[]{:S(2)}, u32[]{:S(2)}) collective-permute-start(bf16[8,96,128]{2,1,0:T(8,128)(2,1)S(1)} %get-tuple-element.15), channel_id=1, source_target_pairs={{0,1},{1,2},{2,3},{3,4},{4,5},{5,6},{6,7},{7,8},{8,9},{9,10},{10,1... | collective-permute-start | bytes 589832 | tf_op jit(solution)/shard_map/ppermute | solution.py:353
  10.4 16.9 %collective-permute-start.1 = (bf16[8,96,128]{2,1,0:T(8,128)(2,1)S(1)}, bf16[8,96,128]{2,1,0:T(8,128)(2,1)S(1)}, u32[]{:S(2)}, u32[]{:S(2)}) collective-permute-start(bf16[8,96,128]{2,1,0:T(8,128)(2,1)S(1)} %get-tuple-element.16), channel_id=1, source_target_pairs={{0,480},{1,481},{2,482},{3,483},{4,484},{5,485},{6,486},{7,487},{8... | collective-permute-start | bytes 589832 | tf_op jit(solution)/shard_map/ppermute | solution.py:353
  13.5 16.3 %collective-permute-start.2 = (bf16[8,96,128]{2,1,0:T(8,128)(2,1)S(1)}, bf16[8,96,128]{2,1,0:T(8,128)(2,1)S(1)}, u32[]{:S(2)}, u32[]{:S(2)}) collective-permute-start(bf16[8,96,128]{2,1,0:T(8,128)(2,1)S(1)} %get-tuple-element.17), channel_id=1, source_target_pairs={{0,511},{1,480},{2,481},{3,482},{4,483},{5,484},{6,485},{7,486},{8... | collective-permute-start | bytes 589832 | tf_op jit(solution)/shard_map/ppermute | solution.py:353
  25.4 1.0 %copy-start.9 = (bf16[768,192]{0,1:T(8,128)(2,1)S(1)}, bf16[768,192]{0,1:T(8,128)(2,1)}, u32[]{:S(2)}) copy-start(bf16[768,192]{0,1:T(8,128)(2,1)} %param.18) | copy-start | bytes 884740
  25.4 1.1 %copy-start.11 = (bf16[192,192]{1,0:T(8,128)(2,1)S(1)}, bf16[192,192]{1,0:T(8,128)(2,1)}, u32[]{:S(2)}) copy-start(bf16[192,192]{1,0:T(8,128)(2,1)} %param.15) | copy-start | bytes 221188
  26.3 3.5 %copy-start.1 = (bf16[768,384]{1,0:T(8,128)(2,1)S(1)}, bf16[768,384]{1,0:T(8,128)(2,1)}, u32[]{:S(2)}) copy-start(bf16[768,384]{1,0:T(8,128)(2,1)} %param.20) | copy-start | bytes 1769476
  26.3 3.5 %copy-start.4 = (bf16[192,768]{1,0:T(8,128)(2,1)S(1)}, bf16[192,768]{1,0:T(8,128)(2,1)}, u32[]{:S(2)}) copy-start(bf16[192,768]{1,0:T(8,128)(2,1)} %expand.1) | copy-start | bytes 884740
  26.5 0.8 copy-start.12
  26.5 3.3 %copy-start.6 = (f32[192]{0:T(256)S(1)}, f32[192]{0:T(256)}, u32[]{:S(2)}) copy-start(f32[192]{0:T(256)} %param.16) | copy-start | bytes 2308
  29.8 0.7 copy-start.5
  30.5 44.0 %copy-start.7 = (bf16[384,1152]{1,0:T(8,128)(2,1)S(1)}, bf16[384,1152]{1,0:T(8,128)(2,1)}, u32[]{:S(2)}) copy-start(bf16[384,1152]{1,0:T(8,128)(2,1)} %mixer.3) | copy-start | bytes 2654212
  41.2 9.9 %collective-permute-start.3 = (bf16[8,16,384]{2,1,0:T(8,128)(2,1)S(1)}, bf16[8,16,384]{2,1,0:T(8,128)(2,1)S(1)}, u32[]{:S(2)}, u32[]{:S(2)}) collective-permute-start(bf16[8,16,384]{2,1,0:T(8,128)(2,1)S(1)} %get-tuple-element.19), channel_id=1, source_target_pairs={{1,0},{2,1},{3,2},{4,3},{5,4},{6,5},{7,6},{8,7},{9,8},{10,9},{11,1... | collective-permute-start | bytes 294920 | tf_op jit(solution)/shard_map/ppermute | solution.py:353
  47.3 8.3 %collective-permute-start.4 = (bf16[8,16,384]{2,1,0:T(8,128)(2,1)S(1)}, bf16[8,16,384]{2,1,0:T(8,128)(2,1)S(1)}, u32[]{:S(2)}, u32[]{:S(2)}) collective-permute-start(bf16[8,16,384]{2,1,0:T(8,128)(2,1)S(1)} %get-tuple-element.20), channel_id=1, source_target_pairs={{480,0},{481,1},{482,2},{483,3},{484,4},{485,5},{486,6},{487,7},{4... | collective-permute-start | bytes 294920 | tf_op jit(solution)/shard_map/ppermute | solution.py:353
  49.2 8.7 %collective-permute-start.5 = (bf16[8,16,384]{2,1,0:T(8,128)(2,1)S(1)}, bf16[8,16,384]{2,1,0:T(8,128)(2,1)S(1)}, u32[]{:S(2)}, u32[]{:S(2)}) collective-permute-start(bf16[8,16,384]{2,1,0:T(8,128)(2,1)S(1)} %get-tuple-element.21), channel_id=1, source_target_pairs={{511,0},{480,1},{481,2},{482,3},{483,4},{484,5},{485,6},{486,7},{4... | collective-permute-start | bytes 294920 | tf_op jit(solution)/shard_map/ppermute | solution.py:353
  57.9 16.5 %copy-start.13 = (f32[384]{0:T(512)S(1)}, f32[384]{0:T(512)}, u32[]{:S(2)}) copy-start(f32[384]{0:T(512)} %param.21) | copy-start | bytes 4612
  58.9 10.1 %collective-permute-start.6 = (bf16[8,64,384]{2,1,0:T(8,128)(2,1)}, bf16[8,64,384]{2,1,0:T(8,128)(2,1)S(1)}, u32[]{:S(2)}, u32[]{:S(2)}) collective-permute-start(bf16[8,64,384]{2,1,0:T(8,128)(2,1)} %assemble.1.mine_ref), channel_id=1, source_target_pairs={{0,32},{1,33},{2,34},{3,35},{4,36},{5,37},{6,38},{7,39},{8,40},{9,... | collective-permute-start | bytes 1179656 | tf_op jit(solution)/shard_map/ppermute | solution.py:353
  60.8 13.6 %collective-permute-start.8 = (bf16[8,64,384]{2,1,0:T(8,128)(2,1)}, bf16[8,64,384]{2,1,0:T(8,128)(2,1)S(1)}, u32[]{:S(2)}, u32[]{:S(2)}) collective-permute-start(bf16[8,64,384]{2,1,0:T(8,128)(2,1)} %assemble.1.mine_ref), channel_id=1, source_target_pairs={{0,1},{1,0},{2,3},{3,2},{4,5},{5,4},{6,7},{7,6},{8,9},{9,8},{10,11... | collective-permute-start | bytes 1179656 | tf_op jit(solution)/shard_map/ppermute | solution.py:353
  69.0 12.2 %collective-permute-start.7 = (bf16[8,64,384]{2,1,0:T(8,128)(2,1)S(1)}, bf16[8,64,384]{2,1,0:T(8,128)(2,1)S(1)}, u32[]{:S(2)}, u32[]{:S(2)}) collective-permute-start(bf16[8,64,384]{2,1,0:T(8,128)(2,1)S(1)} %collective-permute-done.6.a_ref), channel_id=1, source_target_pairs={{0,1},{1,0},{2,3},{3,2},{4,5},{5,4},{6,7},{7,6},{8,9},{9,8},{10,11... | collective-permute-start | bytes 1179656 | tf_op jit(solution)/shard_map/ppermute | solution.py:353
  74.5 1.0 %copy-start.2 = (bf16[8,64,384]{2,1,0:T(8,128)(2,1)S(1)}, bf16[8,64,384]{2,1,0:T(8,128)(2,1)}, u32[]{:S(2)}) copy-start(bf16[8,64,384]{2,1,0:T(8,128)(2,1)} %assemble.1.mine_ref) | copy-start | bytes 1179652
  75.5 5.7 %copy-start.3 = (bf16[8,64,384]{2,1,0:T(8,128)(2,1)S(1)}, bf16[8,64,384]{2,1,0:T(8,128)(2,1)}, u32[]{:S(2)}) copy-start(bf16[8,64,384]{2,1,0:T(8,128)(2,1)} %assemble.1.mine_ref) | copy-start | bytes 1179652
  75.5 5.7 %copy-start.8 = (bf16[384,384]{1,0:T(8,128)(2,1)S(1)}, bf16[384,384]{1,0:T(8,128)(2,1)}, u32[]{:S(2)}) copy-start(bf16[384,384]{1,0:T(8,128)(2,1)} %output.1) | copy-start | bytes 884740
where the time goes:
time: 88.4 us; the launch traced here: 88 us
  starting transfers between devices  43.6 us (49%)
  Pallas kernels  25.5 us (29%)
  waiting for transfers between devices  12.8 us (14%)
  local copies, waits for them, and re-layouts  5.05 us (6%)
  between operations  0.91 us (1%)
    ppermute x9, starting transfers between devices, moved(): return lax.ppermute(value, ('gx', 'gy'), pairs)  43.6 us
    ppermute x9, waiting for transfers between devices, moved(): return lax.ppermute(value, ('gx', 'gy'), pairs)  12.8 us
    pallas_call x2, Pallas kernels, coarse_call(): pl.pallas_call(body, grid=(samples // step,), in_specs=[spec] * len(tiles...  12.5 us
    pallas_call x1, Pallas kernels, fine(): pl.pallas_call(fine_body, grid=(samples // step,), in_specs=[pl.BlockSpec...  10.7 us
    unnamed x30, local copies, waits for them, and re-layouts  4.75 us
  transfers between devices with their start and end apart: 9, of which 4 were waited for; matrix products, arithmetic and copies ran while one was open for 1% of the time, Pallas kernels for 6%

commit v1 on v0

--- a/solution.py
+++ b/solution.py
@@ -133,13 +133,11 @@
     col_ref,
     row_ref,
     diag_ref,
-    gain_window,
+    gains,
     mixer,
     output,
-    gain_hidden,
     expand,
     contract,
-    gain_merge,
     merge_weight,
     own_out,
     col_out,
@@ -160,7 +158,7 @@
         ],
         0,
     )
-    normed = normalize(tokens, gain_window[...]).astype(BF16)
+    normed = normalize(tokens, gains[0:1, :]).astype(BF16)
     mixed = dot(normed, mixer[...]).astype(BF16)
     contexts = []
     for n in range(windows):
@@ -176,7 +174,7 @@
         )
     context = jnp.concatenate(contexts, 0)
     attended = (tokens + dot(context, output[...])).astype(BF16).astype(F32)
-    normed = normalize(attended, gain_hidden[...]).astype(BF16)
+    normed = normalize(attended, gains[1:2, :]).astype(BF16)
     hidden = gelu(dot(normed, expand[...])).astype(BF16)
     refined = (attended + dot(hidden, contract[...])).astype(BF16).astype(F32)
     phases = [
@@ -194,7 +192,7 @@
     spread = sum(jnp.sum(part * part, -1, keepdims=True) for part in centers) / 768.0
     ratio = lax.rsqrt(spread + EPS)
     merged = sum(
-        dot((centers[k] * ratio * gain_merge[k : k + 1, :]).astype(BF16), merge_weight[k])
+        dot((centers[k] * ratio * gains[k + 2 : k + 3, :]).astype(BF16), merge_weight[k])
         for k in range(4)
     ).astype(BF16)
     for n in range(windows):
@@ -244,7 +242,7 @@
         assemble_body,
         in_specs=[pl.BlockSpec(memory_space=pltpu.SMEM)] + [vmem] * 4,
         out_specs=vmem,
-        out_shape=jax.ShapeDtypeStruct((samples, 64, 384), BF16),
+        out_shape=pltpu.VMEM((samples, 64, 384), BF16),
         compiler_params=pltpu.CompilerParams(vmem_limit_bytes=8 << 20),
         name="assemble",
     )(odd, *pieces)
@@ -366,19 +364,18 @@
     row = moved(row, to_row)
     diag = moved(diag, to_diag)
     col = moved(col, to_col)
+    gains = jnp.concatenate([gain_window, gain_hidden, gain_merge]).reshape(6, 192)
     mixer = jnp.pad(mixer_fine.reshape(192, 3, 192), ((0, 0), (0, 0), (0, 64))).reshape(192, 768)
     own, col, row, diag = fine(
         own,
         col,
         row,
         diag,
-        gain_window.reshape(1, 192),
+        gains,
         mixer,
         jnp.pad(output_fine, ((0, 64), (0, 0))),
-        gain_hidden.reshape(1, 192),
         expand,
         contract,
-        gain_merge.reshape(4, 192),
         merge_weight.reshape(4, 192, 384),
     )
     row = moved(row, to_row, True)

time: 88.4 us -> 86.7 us (0.981)
    unnamed x30 -> x27, local copies, waits for them, and re-layouts: 4.75 us -> 3.85 us
  transfers between devices with their start and end apart: 9 -> 9, of which waited for: 4 -> 4; matrix products, arithmetic and copies ran while one was open for 1% -> 2% of each run, Pallas kernels for 6% -> 7%
where the time goes in v1:
time: 86.7 us; the launch traced here: 86.3 us
  starting transfers between devices  43.8 us (51%)
  Pallas kernels  24.8 us (29%)
  waiting for transfers between devices  12.5 us (14%)
  local copies, waits for them, and re-layouts  4.23 us (5%)
  between operations  0.9 us (1%)
    ppermute x9, starting transfers between devices, moved(): return lax.ppermute(value, ('gx', 'gy'), pairs)  43.8 us
    pallas_call x2, Pallas kernels, coarse_call(): pl.pallas_call(body, grid=(samples // step,), in_specs=[spec] * len(tiles...  12.5 us
    ppermute x9, waiting for transfers between devices, moved(): return lax.ppermute(value, ('gx', 'gy'), pairs)  12.5 us
    pallas_call x1, Pallas kernels, fine(): pl.pallas_call(fine_body, grid=(samples // step,), in_specs=[pl.BlockSpec...  10.7 us
    unnamed x27, local copies, waits for them, and re-layouts  3.85 us
  transfers between devices with their start and end apart: 9, of which 4 were waited for; matrix products, arithmetic and copies ran while one was open for 2% of the time, Pallas kernels for 7%

profile of v1, /device:TPU:1, one launch (start us, length us, event | category | flops | bytes accessed | tf_op | source)
XLA Modules:
  0.0 86.3 jit_solution(10128469369626252943)
XLA Ops:
  0.7 1.2 %copy-done = bf16[8,16,16,192]{3,2,1,0:T(8,128)(2,1)S(1)} copy-done((bf16[8,16,16,192]{3,2,1,0:T(8,128)(2,1)S(1)}, bf16[8,16,16,192]{3,2,1,0:T(8,128)(2,1)}, u32[]{:S(2)}) %copy-start) | copy-done | bytes 786456
  1.9 1.3 %pack.1 = (bf16[8,64,192]{2,1,0:T(8,128)(2,1)S(1)}, bf16[8,96,128]{2,1,0:T(8,128)(2,1)S(1)}, bf16[8,96,128]{2,1,0:T(8,128)(2,1)S(1)}, bf16[8,96,128]{2,1,0:T(8,128)(2,1)S(1)}) custom-call(s32[1]{0:T(128)} %bitcast.odd_ref, bf16[8,16,16,192]{3,2,1,0:T(8,128)(2,1)S(1)} %copy-done), custom_call_target="tpu_custom_call" | custom-call | tf_op jit(solution)/shard_map/pack/pallas_call | solution.py:70
  3.2 7.2 %collective-permute-start = (bf16[8,96,128]{2,1,0:T(8,128)(2,1)S(1)}, bf16[8,96,128]{2,1,0:T(8,128)(2,1)S(1)}, u32[]{:S(2)}, u32[]{:S(2)}) collective-permute-start(bf16[8,96,128]{2,1,0:T(8,128)(2,1)S(1)} %get-tuple-element.15), channel_id=1, source_target_pairs={{0,1},{1,2},{2,3},{3,4},{4,5},{5,6},{6,7},{7,8},{8,9},{9,10},{10,1... | collective-permute-start | bytes 589832 | tf_op jit(solution)/shard_map/ppermute | solution.py:351
  10.4 3.1 %collective-permute-start.1 = (bf16[8,96,128]{2,1,0:T(8,128)(2,1)S(1)}, bf16[8,96,128]{2,1,0:T(8,128)(2,1)S(1)}, u32[]{:S(2)}, u32[]{:S(2)}) collective-permute-start(bf16[8,96,128]{2,1,0:T(8,128)(2,1)S(1)} %get-tuple-element.16), channel_id=1, source_target_pairs={{0,480},{1,481},{2,482},{3,483},{4,484},{5,485},{6,486},{7,487},{8... | collective-permute-start | bytes 589832 | tf_op jit(solution)/shard_map/ppermute | solution.py:351
  13.5 11.6 %collective-permute-start.2 = (bf16[8,96,128]{2,1,0:T(8,128)(2,1)S(1)}, bf16[8,96,128]{2,1,0:T(8,128)(2,1)S(1)}, u32[]{:S(2)}, u32[]{:S(2)}) collective-permute-start(bf16[8,96,128]{2,1,0:T(8,128)(2,1)S(1)} %get-tuple-element.17), channel_id=1, source_target_pairs={{0,511},{1,480},{2,481},{3,482},{4,483},{5,484},{6,485},{7,486},{8... | collective-permute-start | bytes 589832 | tf_op jit(solution)/shard_map/ppermute | solution.py:351
  25.1 0.2 copy.15
  25.5 0.8 copy-done.5
  26.3 0.2 copy.17.contract
  26.6 0.7 copy-done.8
  27.5 2.4 %collective-permute-done.2.diag_ref = bf16[8,96,128]{2,1,0:T(8,128)(2,1)S(1)} collective-permute-done((bf16[8,96,128]{2,1,0:T(8,128)(2,1)S(1)}, bf16[8,96,128]{2,1,0:T(8,128)(2,1)S(1)}, u32[]{:S(2)}, u32[]{:S(2)}) %collective-permute-start.2) | collective-permute-done | bytes 196640 | tf_op jit(solution)/shard_map/ppermute | solution.py:351
  29.8 10.7 %fine.1 = (bf16[8,16,384]{2,1,0:T(8,128)(2,1)S(1)}, bf16[8,16,384]{2,1,0:T(8,128)(2,1)S(1)}, bf16[8,16,384]{2,1,0:T(8,128)(2,1)S(1)}, bf16[8,16,384]{2,1,0:T(8,128)(2,1)S(1)}) custom-call(bf16[8,64,192]{2,1,0:T(8,128)(2,1)S(1)} %get-tuple-element.14.own_ref, bf16[8,96,128]{2,1,0:T(8,128)(2,1)S(1)} %collective-permute-done.col_ref, ...), custom_call_target="tpu_custom_call" | custom-call | tf_op jit(solution)/shard_map/fine/pallas_call | solution.py:211
  40.6 6.2 %collective-permute-start.3 = (bf16[8,16,384]{2,1,0:T(8,128)(2,1)S(1)}, bf16[8,16,384]{2,1,0:T(8,128)(2,1)S(1)}, u32[]{:S(2)}, u32[]{:S(2)}) collective-permute-start(bf16[8,16,384]{2,1,0:T(8,128)(2,1)S(1)} %get-tuple-element.19), channel_id=1, source_target_pairs={{1,0},{2,1},{3,2},{4,3},{5,4},{6,5},{7,6},{8,7},{9,8},{10,9},{11,1... | collective-permute-start | bytes 294920 | tf_op jit(solution)/shard_map/ppermute | solution.py:351
  46.7 1.9 %collective-permute-start.4 = (bf16[8,16,384]{2,1,0:T(8,128)(2,1)S(1)}, bf16[8,16,384]{2,1,0:T(8,128)(2,1)S(1)}, u32[]{:S(2)}, u32[]{:S(2)}) collective-permute-start(bf16[8,16,384]{2,1,0:T(8,128)(2,1)S(1)} %get-tuple-element.20), channel_id=1, source_target_pairs={{480,0},{481,1},{482,2},{483,3},{484,4},{485,5},{486,6},{487,7},{4... | collective-permute-start | bytes 294920 | tf_op jit(solution)/shard_map/ppermute | solution.py:351
  48.7 1.9 %collective-permute-start.5 = (bf16[8,16,384]{2,1,0:T(8,128)(2,1)S(1)}, bf16[8,16,384]{2,1,0:T(8,128)(2,1)S(1)}, u32[]{:S(2)}, u32[]{:S(2)}) collective-permute-start(bf16[8,16,384]{2,1,0:T(8,128)(2,1)S(1)} %get-tuple-element.21), channel_id=1, source_target_pairs={{511,0},{480,1},{481,2},{482,3},{483,4},{484,5},{485,6},{486,7},{4... | collective-permute-start | bytes 294920 | tf_op jit(solution)/shard_map/ppermute | solution.py:351
  50.6 4.5 %collective-permute-done.4.row_ref = bf16[8,16,384]{2,1,0:T(8,128)(2,1)S(1)} collective-permute-done((bf16[8,16,384]{2,1,0:T(8,128)(2,1)S(1)}, bf16[8,16,384]{2,1,0:T(8,128)(2,1)S(1)}, u32[]{:S(2)}, u32[]{:S(2)}) %collective-permute-start.4) | collective-permute-done | bytes 98336 | tf_op jit(solution)/shard_map/ppermute | solution.py:351
  55.1 2.3 %collective-permute-done.5.diag_ref = bf16[8,16,384]{2,1,0:T(8,128)(2,1)S(1)} collective-permute-done((bf16[8,16,384]{2,1,0:T(8,128)(2,1)S(1)}, bf16[8,16,384]{2,1,0:T(8,128)(2,1)S(1)}, u32[]{:S(2)}, u32[]{:S(2)}) %collective-permute-start.5) | collective-permute-done | bytes 98336 | tf_op jit(solution)/shard_map/ppermute | solution.py:351
  57.4 0.3 assemble.1.mine_ref
  57.6 1.9 %collective-permute-start.6 = (bf16[8,64,384]{2,1,0:T(8,128)(2,1)S(1)}, bf16[8,64,384]{2,1,0:T(8,128)(2,1)S(1)}, u32[]{:S(2)}, u32[]{:S(2)}) collective-permute-start(bf16[8,64,384]{2,1,0:T(8,128)(2,1)S(1)} %assemble.1.mine_ref), channel_id=1, source_target_pairs={{0,32},{1,33},{2,34},{3,35},{4,36},{5,37},{6,38},{7,39},{8,40},{9,... | collective-permute-start | bytes 1179656 | tf_op jit(solution)/shard_map/ppermute | solution.py:351
  59.6 4.6 %collective-permute-start.8 = (bf16[8,64,384]{2,1,0:T(8,128)(2,1)S(1)}, bf16[8,64,384]{2,1,0:T(8,128)(2,1)S(1)}, u32[]{:S(2)}, u32[]{:S(2)}) collective-permute-start(bf16[8,64,384]{2,1,0:T(8,128)(2,1)S(1)} %assemble.1.mine_ref), channel_id=1, source_target_pairs={{0,1},{1,0},{2,3},{3,2},{4,5},{5,4},{6,7},{7,6},{8,9},{9,8},{10,11... | collective-permute-start | bytes 1179656 | tf_op jit(solution)/shard_map/ppermute | solution.py:351
  64.2 3.4 %collective-permute-done.6.a_ref = bf16[8,64,384]{2,1,0:T(8,128)(2,1)S(1)} collective-permute-done((bf16[8,64,384]{2,1,0:T(8,128)(2,1)S(1)}, bf16[8,64,384]{2,1,0:T(8,128)(2,1)S(1)}, u32[]{:S(2)}, u32[]{:S(2)}) %collective-permute-start.6) | collective-permute-done | bytes 393248 | tf_op jit(solution)/shard_map/ppermute | solution.py:351
  67.5 5.4 %collective-permute-start.7 = (bf16[8,64,384]{2,1,0:T(8,128)(2,1)S(1)}, bf16[8,64,384]{2,1,0:T(8,128)(2,1)S(1)}, u32[]{:S(2)}, u32[]{:S(2)}) collective-permute-start(bf16[8,64,384]{2,1,0:T(8,128)(2,1)S(1)} %collective-permute-done.6.a_ref), channel_id=1, source_target_pairs={{0,1},{1,0},{2,3},{3,2},{4,5},{5,4},{6,7},{7,6},{8,9},{9,8},{10,11... | collective-permute-start | bytes 1179656 | tf_op jit(solution)/shard_map/ppermute | solution.py:351
  73.0 0.7 copy.19
  73.7 5.7 %shard_map.131 = (bf16[8,64,384]{2,1,0:T(8,128)(2,1)S(1)}, f32[8,64,384]{2,1,0:T(8,128)S(1)}, f32[8,64,384]{2,1,0:T(8,128)S(1)}, f32[8,64,384]{2,1,0:T(8,128)S(1)}) custom-call(bf16[8,64,384]{2,1,0:T(8,128)(2,1)S(1)} %assemble.1.mine_ref, bf16[8,64,384]{2,1,0:T(8,128)(2,1)S(1)} %collective-permute-done.8.twin_ref, f32[1,384]{1,0:T(1,128)S(1)} %reshape.34.gain, ...), custom_call_target="tpu_custom_call" | custom-call | flops 2000000000 | bytes 4000000 | tf_op jit(solution)/shard_map/pallas_call | solution.py:313
  79.5 6.8 %shard_map.132 = bf16[8,64,384]{2,1,0:T(8,128)(2,1)} custom-call(bf16[8,64,384]{2,1,0:T(8,128)(2,1)S(1)} %assemble.1.mine_ref, bf16[8,64,384]{2,1,0:T(8,128)(2,1)S(1)} %collective-permute-done.6.a_ref, bf16[8,64,384]{2,1,0:T(8,128)(2,1)S(1)} %collective-permute-done.7.b_ref, bf16[8,64,384]{2,1,0:T(8,128)(2,1)S(1)} %get-tuple-element.22.query_ref, ...), custom_call_target="tpu_custom_call" | custom-call | flops 2000000000 | bytes 4000000 | tf_op jit(solution)/shard_map/pallas_call | solution.py:313
  (32 shorter events, 0.5 us)
Async XLA Ops:
  0.6 1.2 %copy-start = (bf16[8,16,16,192]{3,2,1,0:T(8,128)(2,1)S(1)}, bf16[8,16,16,192]{3,2,1,0:T(8,128)(2,1)}, u32[]{:S(2)}) copy-start(bf16[8,16,16,192]{3,2,1,0:T(8,128)(2,1)} %x_ref.1) | copy-start | bytes 2359300
  1.9 23.3 %copy-start.6 = (bf16[192,576]{1,0:T(8,128)(2,1)S(1)}, bf16[192,576]{1,0:T(8,128)(2,1)}, u32[]{:S(2)}) copy-start(bf16[192,576]{1,0:T(8,128)(2,1)} %param.14) | copy-start | bytes 663556
  3.2 24.2 %collective-permute-start = (bf16[8,96,128]{2,1,0:T(8,128)(2,1)S(1)}, bf16[8,96,128]{2,1,0:T(8,128)(2,1)S(1)}, u32[]{:S(2)}, u32[]{:S(2)}) collective-permute-start(bf16[8,96,128]{2,1,0:T(8,128)(2,1)S(1)} %get-tuple-element.15), channel_id=1, source_target_pairs={{0,1},{1,2},{2,3},{3,4},{4,5},{5,6},{6,7},{7,8},{8,9},{9,10},{10,1... | collective-permute-start | bytes 589832 | tf_op jit(solution)/shard_map/ppermute | solution.py:351
  10.4 17.0 %collective-permute-start.1 = (bf16[8,96,128]{2,1,0:T(8,128)(2,1)S(1)}, bf16[8,96,128]{2,1,0:T(8,128)(2,1)S(1)}, u32[]{:S(2)}, u32[]{:S(2)}) collective-permute-start(bf16[8,96,128]{2,1,0:T(8,128)(2,1)S(1)} %get-tuple-element.16), channel_id=1, source_target_pairs={{0,480},{1,481},{2,482},{3,483},{4,484},{5,485},{6,486},{7,487},{8... | collective-permute-start | bytes 589832 | tf_op jit(solution)/shard_map/ppermute | solution.py:351
  13.5 16.3 %collective-permute-start.2 = (bf16[8,96,128]{2,1,0:T(8,128)(2,1)S(1)}, bf16[8,96,128]{2,1,0:T(8,128)(2,1)S(1)}, u32[]{:S(2)}, u32[]{:S(2)}) collective-permute-start(bf16[8,96,128]{2,1,0:T(8,128)(2,1)S(1)} %get-tuple-element.17), channel_id=1, source_target_pairs={{0,511},{1,480},{2,481},{3,482},{4,483},{5,484},{6,485},{7,486},{8... | collective-permute-start | bytes 589832 | tf_op jit(solution)/shard_map/ppermute | solution.py:351
  25.4 1.0 %copy-start.5 = (bf16[768,192]{0,1:T(8,128)(2,1)S(1)}, bf16[768,192]{0,1:T(8,128)(2,1)}, u32[]{:S(2)}) copy-start(bf16[768,192]{0,1:T(8,128)(2,1)} %param.18) | copy-start | bytes 884740
  25.4 1.1 %copy-start.7 = (bf16[192,192]{1,0:T(8,128)(2,1)S(1)}, bf16[192,192]{1,0:T(8,128)(2,1)}, u32[]{:S(2)}) copy-start(bf16[192,192]{1,0:T(8,128)(2,1)} %param.15) | copy-start | bytes 221188
  26.3 3.5 %copy-start.1 = (bf16[768,384]{1,0:T(8,128)(2,1)S(1)}, bf16[768,384]{1,0:T(8,128)(2,1)}, u32[]{:S(2)}) copy-start(bf16[768,384]{1,0:T(8,128)(2,1)} %param.20) | copy-start | bytes 1769476
  26.3 3.5 %copy-start.2 = (bf16[192,768]{1,0:T(8,128)(2,1)S(1)}, bf16[192,768]{1,0:T(8,128)(2,1)}, u32[]{:S(2)}) copy-start(bf16[192,768]{1,0:T(8,128)(2,1)} %expand.1) | copy-start | bytes 884740
  26.5 0.8 copy-start.8
  26.5 0.8 copy-start.10
  26.5 0.8 copy-start.11
  29.8 43.1 %copy-start.9 = (f32[384]{0:T(512)S(1)}, f32[384]{0:T(512)}, u32[]{:S(2)}) copy-start(f32[384]{0:T(512)} %param.21) | copy-start | bytes 4612
  40.5 33.2 %copy-start.3 = (bf16[384,1152]{1,0:T(8,128)(2,1)S(1)}, bf16[384,1152]{1,0:T(8,128)(2,1)}, u32[]{:S(2)}) copy-start(bf16[384,1152]{1,0:T(8,128)(2,1)} %mixer.3) | copy-start | bytes 2654212
  40.6 10.0 %collective-permute-start.3 = (bf16[8,16,384]{2,1,0:T(8,128)(2,1)S(1)}, bf16[8,16,384]{2,1,0:T(8,128)(2,1)S(1)}, u32[]{:S(2)}, u32[]{:S(2)}) collective-permute-start(bf16[8,16,384]{2,1,0:T(8,128)(2,1)S(1)} %get-tuple-element.19), channel_id=1, source_target_pairs={{1,0},{2,1},{3,2},{4,3},{5,4},{6,5},{7,6},{8,7},{9,8},{10,9},{11,1... | collective-permute-start | bytes 294920 | tf_op jit(solution)/shard_map/ppermute | solution.py:351
  46.7 8.3 %collective-permute-start.4 = (bf16[8,16,384]{2,1,0:T(8,128)(2,1)S(1)}, bf16[8,16,384]{2,1,0:T(8,128)(2,1)S(1)}, u32[]{:S(2)}, u32[]{:S(2)}) collective-permute-start(bf16[8,16,384]{2,1,0:T(8,128)(2,1)S(1)} %get-tuple-element.20), channel_id=1, source_target_pairs={{480,0},{481,1},{482,2},{483,3},{484,4},{485,5},{486,6},{487,7},{4... | collective-permute-start | bytes 294920 | tf_op jit(solution)/shard_map/ppermute | solution.py:351
  48.7 8.7 %collective-permute-start.5 = (bf16[8,16,384]{2,1,0:T(8,128)(2,1)S(1)}, bf16[8,16,384]{2,1,0:T(8,128)(2,1)S(1)}, u32[]{:S(2)}, u32[]{:S(2)}) collective-permute-start(bf16[8,16,384]{2,1,0:T(8,128)(2,1)S(1)} %get-tuple-element.21), channel_id=1, source_target_pairs={{511,0},{480,1},{481,2},{482,3},{483,4},{484,5},{485,6},{486,7},{4... | collective-permute-start | bytes 294920 | tf_op jit(solution)/shard_map/ppermute | solution.py:351
  57.6 9.9 %collective-permute-start.6 = (bf16[8,64,384]{2,1,0:T(8,128)(2,1)S(1)}, bf16[8,64,384]{2,1,0:T(8,128)(2,1)S(1)}, u32[]{:S(2)}, u32[]{:S(2)}) collective-permute-start(bf16[8,64,384]{2,1,0:T(8,128)(2,1)S(1)} %assemble.1.mine_ref), channel_id=1, source_target_pairs={{0,32},{1,33},{2,34},{3,35},{4,36},{5,37},{6,38},{7,39},{8,40},{9,... | collective-permute-start | bytes 1179656 | tf_op jit(solution)/shard_map/ppermute | solution.py:351
  59.6 14.2 %collective-permute-start.8 = (bf16[8,64,384]{2,1,0:T(8,128)(2,1)S(1)}, bf16[8,64,384]{2,1,0:T(8,128)(2,1)S(1)}, u32[]{:S(2)}, u32[]{:S(2)}) collective-permute-start(bf16[8,64,384]{2,1,0:T(8,128)(2,1)S(1)} %assemble.1.mine_ref), channel_id=1, source_target_pairs={{0,1},{1,0},{2,3},{3,2},{4,5},{5,4},{6,7},{7,6},{8,9},{9,8},{10,11... | collective-permute-start | bytes 1179656 | tf_op jit(solution)/shard_map/ppermute | solution.py:351
  67.5 12.0 %collective-permute-start.7 = (bf16[8,64,384]{2,1,0:T(8,128)(2,1)S(1)}, bf16[8,64,384]{2,1,0:T(8,128)(2,1)S(1)}, u32[]{:S(2)}, u32[]{:S(2)}) collective-permute-start(bf16[8,64,384]{2,1,0:T(8,128)(2,1)S(1)} %collective-permute-done.6.a_ref), channel_id=1, source_target_pairs={{0,1},{1,0},{2,3},{3,2},{4,5},{5,4},{6,7},{7,6},{8,9},{9,8},{10,11... | collective-permute-start | bytes 1179656 | tf_op jit(solution)/shard_map/ppermute | solution.py:351
  73.7 5.8 %copy-start.4 = (bf16[384,384]{1,0:T(8,128)(2,1)S(1)}, bf16[384,384]{1,0:T(8,128)(2,1)}, u32[]{:S(2)}) copy-start(bf16[384,384]{1,0:T(8,128)(2,1)} %output.1) | copy-start | bytes 884740

commit v2 on v1

--- a/solution.py
+++ b/solution.py
@@ -64,7 +64,7 @@
 
 def pack(odd, fields):
     samples = fields.shape[0]
-    step = 2
+    step = samples
     piece = jax.ShapeDtypeStruct((samples, 96, 128), BF16)
     piece_spec = pl.BlockSpec((step, 96, 128), lambda n: (n, 0, 0))
     return pl.pallas_call(
@@ -94,34 +94,39 @@
     return jnp.where(jnp.minimum(lane, last) == head, 1.0, 0.0).astype(BF16)
 
 
-def attend_group(queries, keys, values, heads):
-    rows = queries.shape[0]
-    length = keys.shape[0]
+def score(queries, keys, heads):
     masks = [head_mask(head, heads - 1) for head in range(heads)]
     scores = dot_nt(jnp.concatenate([queries * mask for mask in masks], 0), keys)
     highest = jnp.max(scores, -1, keepdims=True) * SCALE
-    power = jnp.exp2(scores * SCALE - highest).astype(BF16)
-    parts = range(heads)
-    powers = [power[head * rows : (head + 1) * rows] for head in parts]
+    return highest, jnp.exp2(scores * SCALE - highest).astype(BF16), masks
+
+
+def attend_whole(queries, keys, values, heads):
+    rows = queries.shape[0]
+    length = keys.shape[0]
+    _, power, masks = score(queries, keys, heads)
+    powers = [power[head * rows : (head + 1) * rows] for head in range(heads)]
     weights = [
         jnp.concatenate([values * mask, jnp.broadcast_to(mask, (length, 128))], 1) for mask in masks
     ]
     sums = dot(jnp.concatenate(powers, 1), jnp.concatenate(weights, 0))
-    return highest, masks, sums[:, :128], sums[:, 128:]
-
-
-def attend_whole(queries, keys, values, heads):
-    _, _, weighted, total = attend_group(queries, keys, values, heads)
-    return (weighted / total).astype(BF16)
+    return (sums[:, :128] / sums[:, 128:]).astype(BF16)
 
 
 def attend_part(queries, keys, values, heads):
     rows = queries.shape[0]
-    highest, masks, weighted, total = attend_group(queries, keys, values, heads)
-    top = sum(
-        highest[head * rows : (head + 1) * rows] * masks[head].astype(F32) for head in range(heads)
-    )
-    return top, weighted, total
+    highest, power, _ = score(queries, keys, heads)
+    sums = dot(power, jnp.concatenate([values, jnp.ones(values.shape, BF16)], 1))
+    lane = iota((1, 128), 1) // HEAD
+
+    def spread(stacked):
+        parts = [stacked[head * rows : (head + 1) * rows] for head in range(heads)]
+        result = jnp.broadcast_to(parts[-1], (rows, 128))
+        for head in reversed(range(heads - 1)):
+            result = jnp.where(lane <= head, parts[head], result)
+        return result
+
+    return spread(highest), spread(sums[:, :128]), spread(sums[:, 128:])
 
 
 def gelu(x):

time: 86.7 us -> 85.6 us (0.987)
  Pallas kernels: 24.8 us -> 23.8 us
where the time goes in v2:
time: 85.6 us; the launch traced here: 85.2 us
  starting transfers between devices  43.8 us (51%)
  Pallas kernels  23.8 us (28%)
  waiting for transfers between devices  12.5 us (15%)
  local copies, waits for them, and re-layouts  4.23 us (5%)
  between operations  0.89 us (1%)
    ppermute x9, starting transfers between devices, moved(): return lax.ppermute(value, ('gx', 'gy'), pairs)  43.8 us
    ppermute x9, waiting for transfers between devices, moved(): return lax.ppermute(value, ('gx', 'gy'), pairs)  12.5 us
    pallas_call x2, Pallas kernels, coarse_call(): pl.pallas_call(body, grid=(samples // step,), in_specs=[spec] * len(tiles...  12.3 us
    pallas_call x1, Pallas kernels, fine(): pl.pallas_call(fine_body, grid=(samples // step,), in_specs=[pl.BlockSpec...  10.8 us
    unnamed x27, local copies, waits for them, and re-layouts  3.85 us
  transfers between devices with their start and end apart: 9, of which 4 were waited for; matrix products, arithmetic and copies ran while one was open for 2% of the time, Pallas kernels for 7%

profile of v2, /device:TPU:1, one launch (start us, length us, event | category | flops | bytes accessed | tf_op | source)
XLA Modules:
  0.0 85.2 jit_solution(2042401572250280723)
XLA Ops:
  0.7 1.2 %copy-done = bf16[8,16,16,192]{3,2,1,0:T(8,128)(2,1)S(1)} copy-done((bf16[8,16,16,192]{3,2,1,0:T(8,128)(2,1)S(1)}, bf16[8,16,16,192]{3,2,1,0:T(8,128)(2,1)}, u32[]{:S(2)}) %copy-start) | copy-done | bytes 786456
  1.9 0.5 pack.1
  2.4 7.2 %collective-permute-start = (bf16[8,96,128]{2,1,0:T(8,128)(2,1)S(1)}, bf16[8,96,128]{2,1,0:T(8,128)(2,1)S(1)}, u32[]{:S(2)}, u32[]{:S(2)}) collective-permute-start(bf16[8,96,128]{2,1,0:T(8,128)(2,1)S(1)} %get-tuple-element.15), channel_id=1, source_target_pairs={{0,1},{1,2},{2,3},{3,4},{4,5},{5,6},{6,7},{7,8},{8,9},{9,10},{10,1... | collective-permute-start | bytes 589832 | tf_op jit(solution)/shard_map/ppermute | solution.py:356
  9.6 3.1 %collective-permute-start.1 = (bf16[8,96,128]{2,1,0:T(8,128)(2,1)S(1)}, bf16[8,96,128]{2,1,0:T(8,128)(2,1)S(1)}, u32[]{:S(2)}, u32[]{:S(2)}) collective-permute-start(bf16[8,96,128]{2,1,0:T(8,128)(2,1)S(1)} %get-tuple-element.16), channel_id=1, source_target_pairs={{0,480},{1,481},{2,482},{3,483},{4,484},{5,485},{6,486},{7,487},{8... | collective-permute-start | bytes 589832 | tf_op jit(solution)/shard_map/ppermute | solution.py:356
  12.7 11.6 %collective-permute-start.2 = (bf16[8,96,128]{2,1,0:T(8,128)(2,1)S(1)}, bf16[8,96,128]{2,1,0:T(8,128)(2,1)S(1)}, u32[]{:S(2)}, u32[]{:S(2)}) collective-permute-start(bf16[8,96,128]{2,1,0:T(8,128)(2,1)S(1)} %get-tuple-element.17), channel_id=1, source_target_pairs={{0,511},{1,480},{2,481},{3,482},{4,483},{5,484},{6,485},{7,486},{8... | collective-permute-start | bytes 589832 | tf_op jit(solution)/shard_map/ppermute | solution.py:356
  24.3 0.2 copy.15
  24.7 0.8 copy-done.5
  25.5 0.2 copy.17.contract
  25.7 0.7 copy-done.8
  26.6 2.4 %collective-permute-done.2.diag_ref = bf16[8,96,128]{2,1,0:T(8,128)(2,1)S(1)} collective-permute-done((bf16[8,96,128]{2,1,0:T(8,128)(2,1)S(1)}, bf16[8,96,128]{2,1,0:T(8,128)(2,1)S(1)}, u32[]{:S(2)}, u32[]{:S(2)}) %collective-permute-start.2) | collective-permute-done | bytes 196640 | tf_op jit(solution)/shard_map/ppermute | solution.py:356
  29.0 10.8 %fine.1 = (bf16[8,16,384]{2,1,0:T(8,128)(2,1)S(1)}, bf16[8,16,384]{2,1,0:T(8,128)(2,1)S(1)}, bf16[8,16,384]{2,1,0:T(8,128)(2,1)S(1)}, bf16[8,16,384]{2,1,0:T(8,128)(2,1)S(1)}) custom-call(bf16[8,64,192]{2,1,0:T(8,128)(2,1)S(1)} %get-tuple-element.14.own_ref, bf16[8,96,128]{2,1,0:T(8,128)(2,1)S(1)} %collective-permute-done.col_ref, ...), custom_call_target="tpu_custom_call" | custom-call | tf_op jit(solution)/shard_map/fine/pallas_call | solution.py:216
  39.8 6.1 %collective-permute-start.3 = (bf16[8,16,384]{2,1,0:T(8,128)(2,1)S(1)}, bf16[8,16,384]{2,1,0:T(8,128)(2,1)S(1)}, u32[]{:S(2)}, u32[]{:S(2)}) collective-permute-start(bf16[8,16,384]{2,1,0:T(8,128)(2,1)S(1)} %get-tuple-element.19), channel_id=1, source_target_pairs={{1,0},{2,1},{3,2},{4,3},{5,4},{6,5},{7,6},{8,7},{9,8},{10,9},{11,1... | collective-permute-start | bytes 294920 | tf_op jit(solution)/shard_map/ppermute | solution.py:356
  45.9 1.9 %collective-permute-start.4 = (bf16[8,16,384]{2,1,0:T(8,128)(2,1)S(1)}, bf16[8,16,384]{2,1,0:T(8,128)(2,1)S(1)}, u32[]{:S(2)}, u32[]{:S(2)}) collective-permute-start(bf16[8,16,384]{2,1,0:T(8,128)(2,1)S(1)} %get-tuple-element.20), channel_id=1, source_target_pairs={{480,0},{481,1},{482,2},{483,3},{484,4},{485,5},{486,6},{487,7},{4... | collective-permute-start | bytes 294920 | tf_op jit(solution)/shard_map/ppermute | solution.py:356
  47.8 1.9 %collective-permute-start.5 = (bf16[8,16,384]{2,1,0:T(8,128)(2,1)S(1)}, bf16[8,16,384]{2,1,0:T(8,128)(2,1)S(1)}, u32[]{:S(2)}, u32[]{:S(2)}) collective-permute-start(bf16[8,16,384]{2,1,0:T(8,128)(2,1)S(1)} %get-tuple-element.21), channel_id=1, source_target_pairs={{511,0},{480,1},{481,2},{482,3},{483,4},{484,5},{485,6},{486,7},{4... | collective-permute-start | bytes 294920 | tf_op jit(solution)/shard_map/ppermute | solution.py:356
  49.8 4.5 %collective-permute-done.4.row_ref = bf16[8,16,384]{2,1,0:T(8,128)(2,1)S(1)} collective-permute-done((bf16[8,16,384]{2,1,0:T(8,128)(2,1)S(1)}, bf16[8,16,384]{2,1,0:T(8,128)(2,1)S(1)}, u32[]{:S(2)}, u32[]{:S(2)}) %collective-permute-start.4) | collective-permute-done | bytes 98336 | tf_op jit(solution)/shard_map/ppermute | solution.py:356
  54.3 2.3 %collective-permute-done.5.diag_ref = bf16[8,16,384]{2,1,0:T(8,128)(2,1)S(1)} collective-permute-done((bf16[8,16,384]{2,1,0:T(8,128)(2,1)S(1)}, bf16[8,16,384]{2,1,0:T(8,128)(2,1)S(1)}, u32[]{:S(2)}, u32[]{:S(2)}) %collective-permute-start.5) | collective-permute-done | bytes 98336 | tf_op jit(solution)/shard_map/ppermute | solution.py:356
  56.5 0.3 assemble.1.mine_ref
  56.8 1.9 %collective-permute-start.6 = (bf16[8,64,384]{2,1,0:T(8,128)(2,1)S(1)}, bf16[8,64,384]{2,1,0:T(8,128)(2,1)S(1)}, u32[]{:S(2)}, u32[]{:S(2)}) collective-permute-start(bf16[8,64,384]{2,1,0:T(8,128)(2,1)S(1)} %assemble.1.mine_ref), channel_id=1, source_target_pairs={{0,32},{1,33},{2,34},{3,35},{4,36},{5,37},{6,38},{7,39},{8,40},{9,... | collective-permute-start | bytes 1179656 | tf_op jit(solution)/shard_map/ppermute | solution.py:356
  58.7 4.6 %collective-permute-start.8 = (bf16[8,64,384]{2,1,0:T(8,128)(2,1)S(1)}, bf16[8,64,384]{2,1,0:T(8,128)(2,1)S(1)}, u32[]{:S(2)}, u32[]{:S(2)}) collective-permute-start(bf16[8,64,384]{2,1,0:T(8,128)(2,1)S(1)} %assemble.1.mine_ref), channel_id=1, source_target_pairs={{0,1},{1,0},{2,3},{3,2},{4,5},{5,4},{6,7},{7,6},{8,9},{9,8},{10,11... | collective-permute-start | bytes 1179656 | tf_op jit(solution)/shard_map/ppermute | solution.py:356
  63.3 3.4 %collective-permute-done.6.a_ref = bf16[8,64,384]{2,1,0:T(8,128)(2,1)S(1)} collective-permute-done((bf16[8,64,384]{2,1,0:T(8,128)(2,1)S(1)}, bf16[8,64,384]{2,1,0:T(8,128)(2,1)S(1)}, u32[]{:S(2)}, u32[]{:S(2)}) %collective-permute-start.6) | collective-permute-done | bytes 393248 | tf_op jit(solution)/shard_map/ppermute | solution.py:356
  66.7 5.4 %collective-permute-start.7 = (bf16[8,64,384]{2,1,0:T(8,128)(2,1)S(1)}, bf16[8,64,384]{2,1,0:T(8,128)(2,1)S(1)}, u32[]{:S(2)}, u32[]{:S(2)}) collective-permute-start(bf16[8,64,384]{2,1,0:T(8,128)(2,1)S(1)} %collective-permute-done.6.a_ref), channel_id=1, source_target_pairs={{0,1},{1,0},{2,3},{3,2},{4,5},{5,4},{6,7},{7,6},{8,9},{9,8},{10,11... | collective-permute-start | bytes 1179656 | tf_op jit(solution)/shard_map/ppermute | solution.py:356
  72.2 0.7 copy.19
  72.9 5.8 %shard_map.131 = (bf16[8,64,384]{2,1,0:T(8,128)(2,1)S(1)}, f32[8,64,384]{2,1,0:T(8,128)S(1)}, f32[8,64,384]{2,1,0:T(8,128)S(1)}, f32[8,64,384]{2,1,0:T(8,128)S(1)}) custom-call(bf16[8,64,384]{2,1,0:T(8,128)(2,1)S(1)} %assemble.1.mine_ref, bf16[8,64,384]{2,1,0:T(8,128)(2,1)S(1)} %collective-permute-done.8.twin_ref, f32[1,384]{1,0:T(1,128)S(1)} %reshape.34.gain, ...), custom_call_target="tpu_custom_call" | custom-call | flops 2000000000 | bytes 4000000 | tf_op jit(solution)/shard_map/pallas_call | solution.py:318
  78.7 6.5 %shard_map.132 = bf16[8,64,384]{2,1,0:T(8,128)(2,1)} custom-call(bf16[8,64,384]{2,1,0:T(8,128)(2,1)S(1)} %assemble.1.mine_ref, bf16[8,64,384]{2,1,0:T(8,128)(2,1)S(1)} %collective-permute-done.6.a_ref, bf16[8,64,384]{2,1,0:T(8,128)(2,1)S(1)} %collective-permute-done.7.b_ref, bf16[8,64,384]{2,1,0:T(8,128)(2,1)S(1)} %get-tuple-element.22.query_ref, ...), custom_call_target="tpu_custom_call" | custom-call | flops 2000000000 | bytes 4000000 | tf_op jit(solution)/shard_map/pallas_call | solution.py:318
  (32 shorter events, 0.5 us)
Async XLA Ops:
  0.6 1.2 %copy-start = (bf16[8,16,16,192]{3,2,1,0:T(8,128)(2,1)S(1)}, bf16[8,16,16,192]{3,2,1,0:T(8,128)(2,1)}, u32[]{:S(2)}) copy-start(bf16[8,16,16,192]{3,2,1,0:T(8,128)(2,1)} %x_ref.1) | copy-start | bytes 2359300
  1.9 22.4 %copy-start.6 = (bf16[192,576]{1,0:T(8,128)(2,1)S(1)}, bf16[192,576]{1,0:T(8,128)(2,1)}, u32[]{:S(2)}) copy-start(bf16[192,576]{1,0:T(8,128)(2,1)} %param.14) | copy-start | bytes 663556
  2.4 24.2 %collective-permute-start = (bf16[8,96,128]{2,1,0:T(8,128)(2,1)S(1)}, bf16[8,96,128]{2,1,0:T(8,128)(2,1)S(1)}, u32[]{:S(2)}, u32[]{:S(2)}) collective-permute-start(bf16[8,96,128]{2,1,0:T(8,128)(2,1)S(1)} %get-tuple-element.15), channel_id=1, source_target_pairs={{0,1},{1,2},{2,3},{3,4},{4,5},{5,6},{6,7},{7,8},{8,9},{9,10},{10,1... | collective-permute-start | bytes 589832 | tf_op jit(solution)/shard_map/ppermute | solution.py:356
  9.6 17.0 %collective-permute-start.1 = (bf16[8,96,128]{2,1,0:T(8,128)(2,1)S(1)}, bf16[8,96,128]{2,1,0:T(8,128)(2,1)S(1)}, u32[]{:S(2)}, u32[]{:S(2)}) collective-permute-start(bf16[8,96,128]{2,1,0:T(8,128)(2,1)S(1)} %get-tuple-element.16), channel_id=1, source_target_pairs={{0,480},{1,481},{2,482},{3,483},{4,484},{5,485},{6,486},{7,487},{8... | collective-permute-start | bytes 589832 | tf_op jit(solution)/shard_map/ppermute | solution.py:356
  12.7 16.3 %collective-permute-start.2 = (bf16[8,96,128]{2,1,0:T(8,128)(2,1)S(1)}, bf16[8,96,128]{2,1,0:T(8,128)(2,1)S(1)}, u32[]{:S(2)}, u32[]{:S(2)}) collective-permute-start(bf16[8,96,128]{2,1,0:T(8,128)(2,1)S(1)} %get-tuple-element.17), channel_id=1, source_target_pairs={{0,511},{1,480},{2,481},{3,482},{4,483},{5,484},{6,485},{7,486},{8... | collective-permute-start | bytes 589832 | tf_op jit(solution)/shard_map/ppermute | solution.py:356
  24.5 1.0 %copy-start.5 = (bf16[768,192]{0,1:T(8,128)(2,1)S(1)}, bf16[768,192]{0,1:T(8,128)(2,1)}, u32[]{:S(2)}) copy-start(bf16[768,192]{0,1:T(8,128)(2,1)} %param.18) | copy-start | bytes 884740
  24.5 1.1 %copy-start.7 = (bf16[192,192]{1,0:T(8,128)(2,1)S(1)}, bf16[192,192]{1,0:T(8,128)(2,1)}, u32[]{:S(2)}) copy-start(bf16[192,192]{1,0:T(8,128)(2,1)} %param.15) | copy-start | bytes 221188
  25.5 3.5 %copy-start.1 = (bf16[768,384]{1,0:T(8,128)(2,1)S(1)}, bf16[768,384]{1,0:T(8,128)(2,1)}, u32[]{:S(2)}) copy-start(bf16[768,384]{1,0:T(8,128)(2,1)} %param.20) | copy-start | bytes 1769476
  25.5 3.5 %copy-start.2 = (bf16[192,768]{1,0:T(8,128)(2,1)S(1)}, bf16[192,768]{1,0:T(8,128)(2,1)}, u32[]{:S(2)}) copy-start(bf16[192,768]{1,0:T(8,128)(2,1)} %expand.1) | copy-start | bytes 884740
  25.7 0.8 copy-start.8
  25.7 0.8 copy-start.10
  25.7 0.8 copy-start.11
  29.0 43.1 %copy-start.9 = (f32[384]{0:T(512)S(1)}, f32[384]{0:T(512)}, u32[]{:S(2)}) copy-start(f32[384]{0:T(512)} %param.21) | copy-start | bytes 4612
  39.8 33.2 %copy-start.3 = (bf16[384,1152]{1,0:T(8,128)(2,1)S(1)}, bf16[384,1152]{1,0:T(8,128)(2,1)}, u32[]{:S(2)}) copy-start(bf16[384,1152]{1,0:T(8,128)(2,1)} %mixer.3) | copy-start | bytes 2654212
  39.8 10.0 %collective-permute-start.3 = (bf16[8,16,384]{2,1,0:T(8,128)(2,1)S(1)}, bf16[8,16,384]{2,1,0:T(8,128)(2,1)S(1)}, u32[]{:S(2)}, u32[]{:S(2)}) collective-permute-start(bf16[8,16,384]{2,1,0:T(8,128)(2,1)S(1)} %get-tuple-element.19), channel_id=1, source_target_pairs={{1,0},{2,1},{3,2},{4,3},{5,4},{6,5},{7,6},{8,7},{9,8},{10,9},{11,1... | collective-permute-start | bytes 294920 | tf_op jit(solution)/shard_map/ppermute | solution.py:356
  45.9 8.3 %collective-permute-start.4 = (bf16[8,16,384]{2,1,0:T(8,128)(2,1)S(1)}, bf16[8,16,384]{2,1,0:T(8,128)(2,1)S(1)}, u32[]{:S(2)}, u32[]{:S(2)}) collective-permute-start(bf16[8,16,384]{2,1,0:T(8,128)(2,1)S(1)} %get-tuple-element.20), channel_id=1, source_target_pairs={{480,0},{481,1},{482,2},{483,3},{484,4},{485,5},{486,6},{487,7},{4... | collective-permute-start | bytes 294920 | tf_op jit(solution)/shard_map/ppermute | solution.py:356
  47.8 8.7 %collective-permute-start.5 = (bf16[8,16,384]{2,1,0:T(8,128)(2,1)S(1)}, bf16[8,16,384]{2,1,0:T(8,128)(2,1)S(1)}, u32[]{:S(2)}, u32[]{:S(2)}) collective-permute-start(bf16[8,16,384]{2,1,0:T(8,128)(2,1)S(1)} %get-tuple-element.21), channel_id=1, source_target_pairs={{511,0},{480,1},{481,2},{482,3},{483,4},{484,5},{485,6},{486,7},{4... | collective-permute-start | bytes 294920 | tf_op jit(solution)/shard_map/ppermute | solution.py:356
  56.8 9.9 %collective-permute-start.6 = (bf16[8,64,384]{2,1,0:T(8,128)(2,1)S(1)}, bf16[8,64,384]{2,1,0:T(8,128)(2,1)S(1)}, u32[]{:S(2)}, u32[]{:S(2)}) collective-permute-start(bf16[8,64,384]{2,1,0:T(8,128)(2,1)S(1)} %assemble.1.mine_ref), channel_id=1, source_target_pairs={{0,32},{1,33},{2,34},{3,35},{4,36},{5,37},{6,38},{7,39},{8,40},{9,... | collective-permute-start | bytes 1179656 | tf_op jit(solution)/shard_map/ppermute | solution.py:356
  58.7 14.2 %collective-permute-start.8 = (bf16[8,64,384]{2,1,0:T(8,128)(2,1)S(1)}, bf16[8,64,384]{2,1,0:T(8,128)(2,1)S(1)}, u32[]{:S(2)}, u32[]{:S(2)}) collective-permute-start(bf16[8,64,384]{2,1,0:T(8,128)(2,1)S(1)} %assemble.1.mine_ref), channel_id=1, source_target_pairs={{0,1},{1,0},{2,3},{3,2},{4,5},{5,4},{6,7},{7,6},{8,9},{9,8},{10,11... | collective-permute-start | bytes 1179656 | tf_op jit(solution)/shard_map/ppermute | solution.py:356
  66.7 12.0 %collective-permute-start.7 = (bf16[8,64,384]{2,1,0:T(8,128)(2,1)S(1)}, bf16[8,64,384]{2,1,0:T(8,128)(2,1)S(1)}, u32[]{:S(2)}, u32[]{:S(2)}) collective-permute-start(bf16[8,64,384]{2,1,0:T(8,128)(2,1)S(1)} %collective-permute-done.6.a_ref), channel_id=1, source_target_pairs={{0,1},{1,0},{2,3},{3,2},{4,5},{5,4},{6,7},{7,6},{8,9},{9,8},{10,11... | collective-permute-start | bytes 1179656 | tf_op jit(solution)/shard_map/ppermute | solution.py:356
  72.9 5.8 %copy-start.4 = (bf16[384,384]{1,0:T(8,128)(2,1)S(1)}, bf16[384,384]{1,0:T(8,128)(2,1)}, u32[]{:S(2)}) copy-start(bf16[384,384]{1,0:T(8,128)(2,1)} %output.1) | copy-start | bytes 884740
